TPU v7x, 32 devices: a whole 2x2x4 slice. The times are simulated.
32 devices in a mesh: fsdp: 4 (over z), tp: 4 (over y, x), job: 2 (over core).
Axes of the slice: x: 2, y: 2, z: 4, core: 2. Of those that a mesh axis runs over, the one named last changes fastest.
Arguments:
- slopes_in: float32 [128, 128, 1024], P('job', 'fsdp', 'tp'), parts along dimension 0, may hold values from -6 to 6
- moments_in: float32 [128, 128, 1024], P('job', 'fsdp', 'tp'), parts along dimension 0, may hold values from -6 to 6
- weights_in: float32 [128, 128, 1024], P('job', 'fsdp', 'tp'), parts along dimension 0, may hold values from -0.1875 to 0.1875
Outputs:
- new_weights: float32 [128, 128, 1024], P('job', 'fsdp', 'tp'), parts along dimension 0
- new_momentum: float32 [128, 128, 1024], P('job', 'fsdp', 'tp'), parts along dimension 0
There are 2 independent parts, one for each index of `job`. A program takes and returns all parts, laid end to end along the dimension named above; each array names one. Nothing has to cross between parts.
All inputs are finite; a program needn't handle non-finite values.
Results may differ from a plain program's by a relative error of at most 0.00019.
Values sent between devices are 32-bit elements; how exact they have to be, the bound alone decides.
A program may use at most 128 MiB of HBM per device.

v0:
```python
import jax
import jax.numpy as jnp
from jax import lax
from jax.sharding import PartitionSpec as P

ITERS = 5
hold_rate = 0.9
learn_rate = 0.8


def body(slopes_in, moments_in, weights_in):
    new_momentum = hold_rate * moments_in + slopes_in
    moved = lax.all_to_all(new_momentum, "fsdp", split_axis=0, concat_axis=1, tiled=True)
    whole = lax.all_to_all(moved, "tp", split_axis=0, concat_axis=2, tiled=True)
    iterate = whole * lax.rsqrt(jnp.sum(whole * whole, axis=(1, 2), keepdims=True) + 1e-06)
    for step in range(ITERS):
        gram = jnp.einsum("mik,mjk->mij", iterate, iterate, precision=lax.Precision.HIGHEST)
        mixed = -4.775 * gram + 2.0315 * jnp.einsum(
            "mij,mjk->mik", gram, gram, precision=lax.Precision.HIGHEST
        )
        iterate = 3.4445 * iterate + jnp.einsum(
            "mij,mjk->mik", mixed, iterate, precision=lax.Precision.HIGHEST
        )
    iterate = lax.all_to_all(iterate, "tp", split_axis=2, concat_axis=0, tiled=True)
    back = lax.all_to_all(iterate, "fsdp", split_axis=1, concat_axis=0, tiled=True)
    new_weights = weights_in - learn_rate * back
    return (new_weights, new_momentum)


def solution(mesh):
    placed = (P("job", "fsdp", "tp"), P("job", "fsdp", "tp"), P("job", "fsdp", "tp"))
    return jax.shard_map(
        body,
        mesh=mesh,
        in_specs=placed,
        out_specs=(P("job", "fsdp", "tp"), P("job", "fsdp", "tp")),
        check_vma=False,
    )
```

profile of v0, /device:TPU:0, one launch (start us, length us, event | category | flops | bytes accessed | tf_op | source)
XLA Modules:
  0.0 195.7 jit_solution(11048177467592807245)
XLA Ops:
  0.6 2.7 %multiply_add_fusion.5 = f32[64,32,256]{2,1,0:T(8,128)S(1)} fusion(f32[64,32,256]{2,1,0:T(8,128)} %param.3, f32[64,32,256]{2,1,0:T(8,128)} %param.4), kind=kLoop, calls=%fused_computation.8 | loop fusion | flops 1048576 | bytes 6291456 | tf_op jit(solution)/shard_map/add | solution.py:12
  3.3 0.0 copy-start
  3.3 54.3 %all_to_all.63 = f32[64,32,256]{2,1,0:T(8,128)S(1)} all-to-all(f32[64,32,256]{2,1,0:T(8,128)S(1)} %multiply_add_fusion.5), channel_id=1, replica_groups=mesh['fsdp'=4,'tp'=4,'job'=2] {'fsdp'}, dimensions={0} | all-to-all | bytes 4194304 | tf_op jit(solution)/shard_map/all_to_all | solution.py:13
  57.7 0.0 copy-done
  57.7 0.1 copy.17
  57.8 27.8 %all_to_all.64 = f32[16,128,256]{2,1,0:T(8,128)S(1)} all-to-all(f32[16,128,256]{2,1,0:T(8,128)S(1)} %bitcast.49), channel_id=1, replica_groups=mesh['fsdp'=4,'tp'=4,'job'=2] {'tp'}, dimensions={0} | all-to-all | bytes 4194304 | tf_op jit(solution)/shard_map/all_to_all | solution.py:14
  85.6 0.3 multiply_reduce_fusion
  85.9 0.3 copy.25
  86.2 2.3 %fusion.2 = f32[4,128,128]{2,1,0:T(8,128)S(1)} fusion(f32[4,128,1024]{2,1,0:T(8,128)S(1)} %bitcast.45, f32[4]{0:T(128)S(1)} %add_rsqrt_fusion), kind=kOutput, calls=%fused_computation.11 | convolution fusion | flops 805830656 | bytes 2359312 | tf_op jit(solution)/shard_map/mik,mjk->mij/dot_general | solution.py:17
  88.5 0.4 fusion.10
  88.9 2.2 %multiply_add_fusion.4 = f32[4,128,1024]{2,1,0:T(8,128)S(1)} fusion(f32[4,128,1024]{2,1,0:T(8,128)S(1)} %bitcast.46, f32[4,128,128]{2,1,0:T(8,128)S(1)} %fusion.10, f32[4]{0:T(128)S(1)} %add_rsqrt_fusion), kind=kOutput, calls=%fused_computation.6 | convolution fusion | flops 807403520 | bytes 4456464 | tf_op jit(solution)/shard_map/mij,mjk->mik/dot_general | solution.py:21
  91.1 2.1 %fusion.13 = f32[4,128,128]{2,1,0:T(8,128)S(1)} fusion(f32[4,128,1024]{2,1,0:T(8,128)S(1)} %multiply_add_fusion.4), kind=kOutput, calls=%fused_computation.26 | convolution fusion | flops 805306368 | bytes 2359296 | tf_op jit(solution)/shard_map/mik,mjk->mij/dot_general | solution.py:17
  93.1 0.4 fusion.9
  93.5 2.1 %multiply_add_fusion.3 = f32[4,128,1024]{2,1,0:T(8,128)S(1)} fusion(f32[4,128,1024]{2,1,0:T(8,128)S(1)} %multiply_add_fusion.4, f32[4,128,128]{2,1,0:T(8,128)S(1)} %fusion.9), kind=kOutput, calls=%fused_computation.5 | convolution fusion | flops 806354944 | bytes 4456448 | tf_op jit(solution)/shard_map/mij,mjk->mik/dot_general | solution.py:21
  95.6 2.1 %fusion.14 = f32[4,128,128]{2,1,0:T(8,128)S(1)} fusion(f32[4,128,1024]{2,1,0:T(8,128)S(1)} %multiply_add_fusion.3), kind=kOutput, calls=%fused_computation.27 | convolution fusion | flops 805306368 | bytes 2359296 | tf_op jit(solution)/shard_map/mik,mjk->mij/dot_general | solution.py:17
  97.6 0.4 fusion.8
  98.0 2.3 %multiply_add_fusion.2 = f32[4,128,1024]{2,1,0:T(8,128)S(1)} fusion(f32[4,128,1024]{2,1,0:T(8,128)S(1)} %multiply_add_fusion.3, f32[4,128,128]{2,1,0:T(8,128)S(1)} %fusion.8), kind=kOutput, calls=%fused_computation.4 | convolution fusion | flops 806354944 | bytes 4456448 | tf_op jit(solution)/shard_map/mij,mjk->mik/dot_general | solution.py:21
  100.3 2.0 %fusion.15 = f32[4,128,128]{2,1,0:T(8,128)S(1)} fusion(f32[4,128,1024]{2,1,0:T(8,128)S(1)} %multiply_add_fusion.2), kind=kOutput, calls=%fused_computation.28 | convolution fusion | flops 805306368 | bytes 2359296 | tf_op jit(solution)/shard_map/mik,mjk->mij/dot_general | solution.py:17
  102.4 0.4 fusion.7
  102.7 2.1 %multiply_add_fusion.1 = f32[4,128,1024]{2,1,0:T(8,128)S(1)} fusion(f32[4,128,1024]{2,1,0:T(8,128)S(1)} %multiply_add_fusion.2, f32[4,128,128]{2,1,0:T(8,128)S(1)} %fusion.7), kind=kOutput, calls=%fused_computation.3 | convolution fusion | flops 806354944 | bytes 4456448 | tf_op jit(solution)/shard_map/mij,mjk->mik/dot_general | solution.py:21
  104.8 2.0 %fusion.16 = f32[4,128,128]{2,1,0:T(8,128)S(1)} fusion(f32[4,128,1024]{2,1,0:T(8,128)S(1)} %multiply_add_fusion.1), kind=kOutput, calls=%fused_computation.29 | convolution fusion | flops 805306368 | bytes 2359296 | tf_op jit(solution)/shard_map/mik,mjk->mij/dot_general | solution.py:17
  106.9 0.4 fusion.6
  107.3 2.1 %multiply_add_fusion = f32[4,128,1024]{2,1,0:T(8,128)S(1)} fusion(f32[4,128,1024]{2,1,0:T(8,128)S(1)} %multiply_add_fusion.1, f32[4,128,128]{2,1,0:T(8,128)S(1)} %fusion.6), kind=kOutput, calls=%fused_computation.2 | convolution fusion | flops 806354944 | bytes 4456448 | tf_op jit(solution)/shard_map/mij,mjk->mik/dot_general | solution.py:21
  109.3 1.8 copy.19
  111.2 26.5 %all_to_all.65 = f32[4,128,1024]{1,0,2:T(4,128)S(1)} all-to-all(f32[4,128,1024]{1,0,2:T(4,128)} %copy.19), channel_id=1, replica_groups=mesh['fsdp'=4,'tp'=4,'job'=2] {'tp'}, dimensions={2} | all-to-all | bytes 4194304 | tf_op jit(solution)/shard_map/all_to_all | solution.py:24
  137.6 0.1 copy.20
  137.8 1.8 copy.21
  139.6 2.8 %copy.22 = f32[16,128,256]{2,0,1:T(8,128)S(1)} copy(f32[16,128,256]{2,1,0:T(8,128)} %bitcast.51) | data formatting | bytes 4194304 | tf_op jit(solution)/shard_map/all_to_all | solution.py:24
  142.4 48.6 %all_to_all.66 = f32[16,128,256]{2,0,1:T(8,128)S(1)} all-to-all(f32[16,128,256]{2,0,1:T(8,128)S(1)} %copy.22), channel_id=1, replica_groups=mesh['fsdp'=4,'tp'=4,'job'=2] {'fsdp'}, dimensions={1} | all-to-all | bytes 4194304 | tf_op jit(solution)/shard_map/all_to_all | solution.py:25
  191.0 1.4 copy_multiply_fusion
  192.4 0.0 copy-start.1
  192.4 0.1 copy.24
  192.5 1.4 copy-done.1
  194.0 1.7 bitcast_subtract_fusion
  (1 shorter events, 0.0 us)
Async XLA Ops:
  3.3 54.4 %copy-start = (f32[64,32,256]{2,1,0:T(8,128)}, f32[64,32,256]{2,1,0:T(8,128)S(1)}, u32[]{:S(2)}) copy-start(f32[64,32,256]{2,1,0:T(8,128)S(1)} %multiply_add_fusion.5) | copy-start | bytes 6291460
  192.4 1.6 copy-start.1
where the time goes:
time: 196 us
  blocking collectives  157 us (80%)
  matrix products  23 us (12%)
  local copies, waits for them, and re-layouts  8.59 us (4%)
  other arithmetic  6.08 us (3%)
    all_to_all x1, blocking collectives, body(): lax.all_to_all(new_momentum, 'fsdp', split_axis=0, concat_axis=1, tiled=T...  54.3 us
    all_to_all x1, blocking collectives, body(): lax.all_to_all(iterate, 'fsdp', split_axis=1, concat_axis=0, tiled=True)  48.6 us
    all_to_all x1, blocking collectives, body(): whole = lax.all_to_all(moved, 'tp', split_axis=0, concat_axis=2, tiled=True)  27.8 us
    all_to_all x1, blocking collectives, body(): lax.all_to_all(iterate, 'tp', split_axis=2, concat_axis=0, tiled=True)  26.5 us
    dot_general x5, matrix products, body(): jnp.einsum('mij,mjk->mik', mixed, iterate, precision=lax.Precision.HIGHEST)  10.7 us
    dot_general x5, matrix products, body(): jnp.einsum('mik,mjk->mij', iterate, iterate, precision=lax.Precision.HIGH...  10.5 us
    all_to_all x3, local copies, waits for them, and re-layouts, body(): lax.all_to_all(iterate, 'tp', split_axis=2, concat_axis=0, tiled=True)  4.76 us

commit v1 on v0

--- a/solution.py
+++ b/solution.py
@@ -21,7 +21,10 @@
         iterate = 3.4445 * iterate + jnp.einsum(
             "mij,mjk->mik", mixed, iterate, precision=lax.Precision.HIGHEST
         )
-    iterate = lax.all_to_all(iterate, "tp", split_axis=2, concat_axis=0, tiled=True)
+    iterate = jnp.concatenate(
+        lax.all_to_all(jnp.stack(jnp.split(iterate, lax.axis_size("tp"), axis=2)), "tp", 0, 0),
+        axis=0,
+    )
     back = lax.all_to_all(iterate, "fsdp", split_axis=1, concat_axis=0, tiled=True)
     new_weights = weights_in - learn_rate * back
     return (new_weights, new_momentum)

time: 196 us -> 189 us (0.964)
  local copies, waits for them, and re-layouts: 8.59 us -> 3.51 us
    all_to_all x3 -> x0, local copies, waits for them, and re-layouts: 4.76 us -> none  [body(): lax.all_to_all(iterate, 'tp', split_axis=2, concat_axis=0, tiled=True)]
where the time goes in v1:
time: 189 us
  blocking collectives  156 us (83%)
  matrix products  23 us (12%)
  other arithmetic  5.12 us (3%)
  local copies, waits for them, and re-layouts  3.51 us (2%)
    all_to_all x1, blocking collectives, body(): lax.all_to_all(new_momentum, 'fsdp', split_axis=0, concat_axis=1, tiled=T...  54.3 us
    all_to_all x1, blocking collectives, body(): lax.all_to_all(iterate, 'fsdp', split_axis=1, concat_axis=0, tiled=True)  48.6 us
    all_to_all x1, blocking collectives, body(): whole = lax.all_to_all(moved, 'tp', split_axis=0, concat_axis=2, tiled=True)  27.8 us
    all_to_all x1, blocking collectives, body(): lax.all_to_all(jnp.stack(jnp.split(iterate, lax.axis_size('tp'), axis=2))...  25.4 us
    dot_general x5, matrix products, body(): jnp.einsum('mij,mjk->mik', mixed, iterate, precision=lax.Precision.HIGHEST)  10.7 us
    dot_general x5, matrix products, body(): jnp.einsum('mik,mjk->mij', iterate, iterate, precision=lax.Precision.HIGH...  10.5 us

profile of v1, /device:TPU:0, one launch (start us, length us, event | category | flops | bytes accessed | tf_op | source)
XLA Modules:
  0.0 188.6 jit_solution(16118599072934997705)
XLA Ops:
  0.6 2.7 %multiply_add_fusion.5 = f32[64,32,256]{2,1,0:T(8,128)S(1)} fusion(f32[64,32,256]{2,1,0:T(8,128)} %param.3, f32[64,32,256]{2,1,0:T(8,128)} %param.4), kind=kLoop, calls=%fused_computation.8 | loop fusion | flops 1048576 | bytes 6291456 | tf_op jit(solution)/shard_map/add | solution.py:12
  3.3 0.0 copy-start
  3.3 54.3 %all_to_all.50 = f32[64,32,256]{2,1,0:T(8,128)S(1)} all-to-all(f32[64,32,256]{2,1,0:T(8,128)S(1)} %multiply_add_fusion.5), channel_id=1, replica_groups=mesh['fsdp'=4,'tp'=4,'job'=2] {'fsdp'}, dimensions={0} | all-to-all | bytes 4194304 | tf_op jit(solution)/shard_map/all_to_all | solution.py:13
  57.7 0.0 copy-done
  57.7 0.2 copy.11
  57.9 27.8 %all_to_all.51 = f32[16,128,256]{2,1,0:T(8,128)S(1)} all-to-all(f32[16,128,256]{2,1,0:T(8,128)S(1)} %bitcast.54), channel_id=1, replica_groups=mesh['fsdp'=4,'tp'=4,'job'=2] {'tp'}, dimensions={0} | all-to-all | bytes 4194304 | tf_op jit(solution)/shard_map/all_to_all | solution.py:14
  85.7 0.3 multiply_reduce_fusion
  86.0 0.2 copy.15
  86.3 2.3 %fusion.2 = f32[4,128,128]{2,1,0:T(8,128)S(1)} fusion(f32[4,128,1024]{2,1,0:T(8,128)S(1)} %bitcast.50, f32[4]{0:T(128)S(1)} %add_rsqrt_fusion), kind=kOutput, calls=%fused_computation.11 | convolution fusion | flops 805830656 | bytes 2359312 | tf_op jit(solution)/shard_map/mik,mjk->mij/dot_general | solution.py:17
  88.5 0.4 fusion.10
  88.9 2.1 %multiply_add_fusion.4 = f32[4,128,1024]{2,1,0:T(8,128)S(1)} fusion(f32[4,128,1024]{2,1,0:T(8,128)S(1)} %bitcast.51, f32[4,128,128]{2,1,0:T(8,128)S(1)} %fusion.10, f32[4]{0:T(128)S(1)} %add_rsqrt_fusion), kind=kOutput, calls=%fused_computation.6 | convolution fusion | flops 807403520 | bytes 4456464 | tf_op jit(solution)/shard_map/mij,mjk->mik/dot_general | solution.py:21
  91.1 2.0 %fusion.13 = f32[4,128,128]{2,1,0:T(8,128)S(1)} fusion(f32[4,128,1024]{2,1,0:T(8,128)S(1)} %multiply_add_fusion.4), kind=kOutput, calls=%fused_computation.31 | convolution fusion | flops 805306368 | bytes 2359296 | tf_op jit(solution)/shard_map/mik,mjk->mij/dot_general | solution.py:17
  93.1 0.4 fusion.9
  93.5 2.1 %multiply_add_fusion.3 = f32[4,128,1024]{2,1,0:T(8,128)S(1)} fusion(f32[4,128,1024]{2,1,0:T(8,128)S(1)} %multiply_add_fusion.4, f32[4,128,128]{2,1,0:T(8,128)S(1)} %fusion.9), kind=kOutput, calls=%fused_computation.5 | convolution fusion | flops 806354944 | bytes 4456448 | tf_op jit(solution)/shard_map/mij,mjk->mik/dot_general | solution.py:21
  95.6 2.0 %fusion.14 = f32[4,128,128]{2,1,0:T(8,128)S(1)} fusion(f32[4,128,1024]{2,1,0:T(8,128)S(1)} %multiply_add_fusion.3), kind=kOutput, calls=%fused_computation.32 | convolution fusion | flops 805306368 | bytes 2359296 | tf_op jit(solution)/shard_map/mik,mjk->mij/dot_general | solution.py:17
  97.6 0.4 fusion.8
  98.0 2.3 %multiply_add_fusion.2 = f32[4,128,1024]{2,1,0:T(8,128)S(1)} fusion(f32[4,128,1024]{2,1,0:T(8,128)S(1)} %multiply_add_fusion.3, f32[4,128,128]{2,1,0:T(8,128)S(1)} %fusion.8), kind=kOutput, calls=%fused_computation.4 | convolution fusion | flops 806354944 | bytes 4456448 | tf_op jit(solution)/shard_map/mij,mjk->mik/dot_general | solution.py:21
  100.3 2.0 %fusion.15 = f32[4,128,128]{2,1,0:T(8,128)S(1)} fusion(f32[4,128,1024]{2,1,0:T(8,128)S(1)} %multiply_add_fusion.2), kind=kOutput, calls=%fused_computation.33 | convolution fusion | flops 805306368 | bytes 2359296 | tf_op jit(solution)/shard_map/mik,mjk->mij/dot_general | solution.py:17
  102.4 0.4 fusion.7
  102.7 2.1 %multiply_add_fusion.1 = f32[4,128,1024]{2,1,0:T(8,128)S(1)} fusion(f32[4,128,1024]{2,1,0:T(8,128)S(1)} %multiply_add_fusion.2, f32[4,128,128]{2,1,0:T(8,128)S(1)} %fusion.7), kind=kOutput, calls=%fused_computation.3 | convolution fusion | flops 806354944 | bytes 4456448 | tf_op jit(solution)/shard_map/mij,mjk->mik/dot_general | solution.py:21
  104.8 2.0 %fusion.16 = f32[4,128,128]{2,1,0:T(8,128)S(1)} fusion(f32[4,128,1024]{2,1,0:T(8,128)S(1)} %multiply_add_fusion.1), kind=kOutput, calls=%fused_computation.34 | convolution fusion | flops 805306368 | bytes 2359296 | tf_op jit(solution)/shard_map/mik,mjk->mij/dot_general | solution.py:17
  106.9 0.4 fusion.6
  107.3 2.1 %multiply_add_fusion = f32[4,128,1024]{2,1,0:T(8,128)S(1)} fusion(f32[4,128,1024]{2,1,0:T(8,128)S(1)} %multiply_add_fusion.1, f32[4,128,128]{2,1,0:T(8,128)S(1)} %fusion.6), kind=kOutput, calls=%fused_computation.2 | convolution fusion | flops 806354944 | bytes 4456448 | tf_op jit(solution)/shard_map/mij,mjk->mik/dot_general | solution.py:21
  109.3 0.2 slice_bitcast_fusion.3
  109.6 0.2 pad_maximum_fusion
  109.8 25.4 %all_to_all.52 = f32[4,4,128,256]{3,2,1,0:T(8,128)S(1)} all-to-all(f32[4,4,128,256]{3,2,1,0:T(8,128)S(1)} %pad_maximum_fusion), channel_id=1, replica_groups=mesh['fsdp'=4,'tp'=4,'job'=2] {'tp'}, dimensions={0} | all-to-all | bytes 4194304 | tf_op jit(solution)/shard_map/all_to_all | solution.py:25
  135.1 1.2 copy.13
  136.3 48.6 %all_to_all.53 = f32[16,128,256]{2,0,1:T(8,128)S(1)} all-to-all(f32[16,128,256]{2,0,1:T(8,128)S(1)} %copy.13), channel_id=1, replica_groups=mesh['fsdp'=4,'tp'=4,'job'=2] {'fsdp'}, dimensions={1} | all-to-all | bytes 4194304 | tf_op jit(solution)/shard_map/all_to_all | solution.py:28
  185.0 0.2 broadcast_multiply_fusion
  185.2 0.0 copy-start.1
  185.3 1.2 copy.14
  186.5 0.4 copy-done.1
  186.8 1.7 bitcast_subtract_fusion
  (1 shorter events, 0.0 us)
Async XLA Ops:
  3.3 54.4 %copy-start = (f32[64,32,256]{2,1,0:T(8,128)}, f32[64,32,256]{2,1,0:T(8,128)S(1)}, u32[]{:S(2)}) copy-start(f32[64,32,256]{2,1,0:T(8,128)S(1)} %multiply_add_fusion.5) | copy-start | bytes 6291460
  185.2 1.6 copy-start.1
